TPU v7x, 32 devices: a whole 2x2x4 slice. The times are simulated.
32 devices in a mesh: row: 8 (over z, x), col: 4 (over y, core).
Axes of the slice: x: 2, y: 2, z: 4, core: 2. Of those that a mesh axis runs over, the one named last changes fastest.
Arguments:
- matrix: float32 [64, 8, 128, 128], P('row', 'col'), may hold values from -0.1875 to 0.1875
- columns: int32 [64, 8], P('row', 'col'), may hold values from 0 to 15
- counts: int32 [64, 4], P('row', 'col'), may hold values from 1 to 2
- fine_guess: float32 [64, 32, 128], P(('col', 'row')), may hold values from -6 to 6
- right_side: float32 [64, 32, 128], P(('row', 'col')), may hold values from -6 to 6
- aggregate: int32 [64], P(('row', 'col')), may hold values from 0 to 7
- restrict: float32 [64, 128, 128], P(('row', 'col')), may hold values from -0.5 to 0.5
Outputs:
- coarse_scaled: float32 [64, 32, 128], P('row')
- residual: float32 [64, 32, 128], P(('row', 'col'))
Inputs may be any that keep to these rules, and one draw needn't show every extreme that they name: `counts`: slots at or past the count hold no part of the operator.
All inputs are finite; a program needn't handle non-finite values.
Results may differ from a plain program's by a relative error of at most 0.000071.
Values sent between devices are 32-bit elements; how exact they have to be, the bound alone decides.
A program may use at most 64 MiB of HBM per device.

v0:
```python
import jax
import jax.numpy as jnp
from jax import lax
from jax.sharding import PartitionSpec as P

NC_GRP = 8


def local(matrix, columns, counts, fine_guess, right_side, aggregate, restrict):
    column_vector = lax.all_gather(fine_guess, "row", axis=0, tiled=True)
    slot_count = matrix.shape[1]
    usable = jnp.arange(slot_count, dtype=jnp.int32)[None, :] < counts
    picked = jnp.take(column_vector, columns, axis=0) * usable[:, :, None, None].astype(jnp.float32)
    partial_value = jnp.einsum("gsab,gsvb->gva", matrix, picked, precision=lax.Precision.HIGHEST)
    product = lax.psum_scatter(partial_value, "col", scatter_dimension=0, tiled=True)
    residual = right_side - product
    contrib = jnp.einsum("gva,gak->gvk", residual, restrict, precision=lax.Precision.HIGHEST)
    onehot = (aggregate[:, None] == jnp.arange(NC_GRP, dtype=jnp.int32)[None, :]).astype(
        jnp.float32
    )
    coarse_part = jnp.einsum("gc,gvk->cvk", onehot, contrib, precision=lax.Precision.HIGHEST)
    squares = jnp.sum(residual * residual, axis=(0, 2))
    coarse = lax.psum(coarse_part, "col")
    total_sq = lax.psum(squares, ("row", "col"))
    entries = residual.shape[0] * residual.shape[2] * lax.axis_size("row") * lax.axis_size("col")
    scale_rms = jnp.sqrt(total_sq / entries + 1e-06)
    return (coarse / scale_rms[None, :, None], residual)


def solution(mesh):
    in_specs = (
        P("row", "col", None, None),
        P("row", "col"),
        P("row", "col"),
        P(("col", "row"), None, None),
        P(("row", "col"), None, None),
        P(("row", "col")),
        P(("row", "col"), None, None),
    )
    out_specs = (P("row", None, None), P(("row", "col"), None, None))
    return jax.shard_map(local, mesh=mesh, in_specs=in_specs, out_specs=out_specs, check_vma=False)
```

profile of v0, /device:TPU:0, one launch (start us, length us, event | category | flops | bytes accessed | tf_op | source)
XLA Modules:
  0.0 115.5 jit_solution(6656684423005813290)
XLA Ops:
  7.2 0.0 copy-start
  7.2 0.0 copy-start.4
  7.2 0.0 reduce-scatter.2.cloned.1.call-start
  7.2 0.8 compare_select_fusion
  8.0 0.0 copy-done.4
  8.0 32.8 %all_gather.3 = f32[16,32,128]{2,1,0:T(8,128)S(1)} all-gather(f32[2,32,128]{2,1,0:T(8,128)} %param.10), channel_id=1, replica_groups=mesh['row'=8,'col'=4] {'row'}, dimensions={0}, use_global_device_ids=true | all-gather | bytes 294912 | tf_op jit(solution)/shard_map/all_gather | solution.py:10
  40.8 0.1 copy.16
  40.9 0.1 reshape.37
  40.9 0.0 copy-start.6
  41.0 0.6 copy-done.6
  41.6 0.1 fusion.7
  41.7 0.1 copy.15
  41.8 0.6 gather_fusion
  42.3 0.0 copy-done
  42.4 0.0 copy-start.3
  42.4 1.9 %convolution_bitcast_fusion = f32[8,32,128]{2,1,0:T(8,128)} fusion(f32[8,2,128,128]{3,2,1,0:T(8,128)S(1)} %copy-done, f32[8,2,32,128]{3,2,1,0:T(8,128)S(1)} %bitcast.11, f32[8,2]{1,0:T(8,128)S(1)} %fusion.7, pred[8,2]{1,0:T(8,128)(4,1)S(1)} %copy.15), kind=kOutput, calls=%fused_computation.1 | convolution fusion | flops 100794368 | bytes 1441872 | tf_op jit(solution)/shard_map/gsab,gsvb->gva/dot_general | solution.py:14
  44.3 0.0 copy-start.1
  44.3 0.0 reduce-scatter.2.cloned.1.call-update
  44.3 0.0 all-reduce.2.cloned.1.call-start
  44.3 20.7 %reduce-scatter.2.cloned.1.call-done = f32[2,32,128]{2,1,0:T(8,128)} async-done(((f32[8,32,128]{2,1,0:T(8,128)}), f32[2,32,128]{2,1,0:T(8,128)}) %reduce-scatter.2.cloned.1.call-update) | async-done | bytes 32784 | tf_op jit(solution)/shard_map/reduce_scatter | solution.py:15
  65.0 0.0 copy-done.3
  65.0 0.9 multiply_reduce_fusion
  65.9 0.0 copy-start.2
  65.9 0.0 copy-done.1
  65.9 0.0 copy-start.5
  65.9 0.2 fusion.13
  66.2 0.4 copy-done.2
  66.5 0.1 copy-done.5
  66.6 1.0 fusion.5
  67.6 0.0 all-reduce.2.cloned.1.call-update
  67.6 39.3 %psum.15 = f32[32]{0:T(128)S(1)} all-reduce(f32[32]{0:T(128)S(1)} %get-tuple-element.8), channel_id=1, replica_groups=mesh['row'=8,'col'=4] {'row','col'}, use_global_device_ids=true, to_apply=%region_3.4 | all-reduce | flops 32 | bytes 256 | tf_op jit(solution)/shard_map/psum | solution.py:24
  106.9 0.0 all-reduce.2.cloned.1.call-done
  107.0 1.0 broadcast_divide_fusion
  108.0 0.7 copy.18
  (3 shorter events, 0.0 us)
Async XLA Ops:
  7.2 35.2 %copy-start = (f32[8,2,128,128]{3,2,1,0:T(8,128)S(1)}, f32[8,2,128,128]{3,2,1,0:T(8,128)}, u32[]{:S(2)}) copy-start(f32[8,2,128,128]{3,2,1,0:T(8,128)} %param.7) | copy-start | bytes 3145732
  7.2 0.8 copy-start.4
  7.2 57.8 %reduce-scatter.2.cloned.1.call-start = ((), (), s32[]{:S(2)}) async-start(), calls=%async_computation.1 | async-start | bytes 163840 | tf_op jit(solution)/shard_map/reduce_scatter | solution.py:15
  40.9 0.7 copy-start.6
  42.4 22.7 %copy-start.3 = (f32[2,32,128]{2,1,0:T(8,128)S(1)}, f32[2,32,128]{2,1,0:T(8,128)}, u32[]{:S(2)}) copy-start(f32[2,32,128]{2,1,0:T(8,128)} %param.11) | copy-start | bytes 98308
  44.3 21.7 %copy-start.1 = (f32[2,128,128]{2,1,0:T(8,128)S(1)}, f32[2,128,128]{2,1,0:T(8,128)}, u32[]{:S(2)}) copy-start(f32[2,128,128]{2,1,0:T(8,128)} %param.13) | copy-start | bytes 393220
  44.3 62.7 %all-reduce.2.cloned.1.call-start = ((), (), s32[]{:S(2)}) async-start(), calls=%async_computation.2 | async-start | bytes 262144 | tf_op jit(solution)/shard_map/psum | solution.py:23
  65.9 0.6 copy-start.2
  65.9 0.7 copy-start.5
Sparse Core Ops, SparseCore 0:
  44.4 20.5 reduce-scatter.1
  67.9 31.7 all-reduce.1
where the time goes:
time: 116 us; the launch traced here: 115 us
  blocking collectives  72.1 us (62%)
  waiting for transfers between devices  20.8 us (18%)
  between operations  14.1 us (12%)
  matrix products  3.07 us (3%)
  other arithmetic  2.73 us (2%)
  local copies, waits for them, and re-layouts  2.62 us (2%)
    psum x1, blocking collectives, local(): total_sq = lax.psum(squares, ('row', 'col'))  39.3 us
    all_gather x1, blocking collectives, local(): column_vector = lax.all_gather(fine_guess, 'row', axis=0, tiled=True)  32.8 us
    reduce_scatter x1, waiting for transfers between devices, local(): lax.psum_scatter(partial_value, 'col', scatter_dimension=0, tiled=True)  20.7 us
  transfers between devices with their start and end apart: 2, of which 1 were waited for; matrix products, arithmetic and copies ran while one was open for 0% of the time, Pallas kernels for 0%

commit v1 on v0

--- a/solution.py
+++ b/solution.py
@@ -21,7 +21,8 @@
     coarse_part = jnp.einsum("gc,gvk->cvk", onehot, contrib, precision=lax.Precision.HIGHEST)
     squares = jnp.sum(residual * residual, axis=(0, 2))
     coarse = lax.psum(coarse_part, "col")
-    total_sq = lax.psum(squares, ("row", "col"))
+    time_entries = lambda piece_in: jnp.sum(jax.lax.all_gather(piece_in, ("row", "col")), axis=0)
+    total_sq = time_entries(squares)
     entries = residual.shape[0] * residual.shape[2] * lax.axis_size("row") * lax.axis_size("col")
     scale_rms = jnp.sqrt(total_sq / entries + 1e-06)
     return (coarse / scale_rms[None, :, None], residual)

time: 116 us -> 116 us (level)
    psum x1 -> x0, blocking collectives: 39.3 us -> none  [local(): total_sq = lax.psum(squares, ('row', 'col'))]
    unnamed x0 -> x1, blocking collectives: none -> 39.3 us
where the time goes in v1:
time: 116 us
  blocking collectives  72.1 us (62%)
  waiting for transfers between devices  20.7 us (18%)
  between operations  14.1 us (12%)
  matrix products  3.07 us (3%)
  local copies, waits for them, and re-layouts  2.94 us (3%)
  other arithmetic  2.76 us (2%)
    unnamed x1, blocking collectives  39.3 us
    all_gather x1, blocking collectives, local(): column_vector = lax.all_gather(fine_guess, 'row', axis=0, tiled=True)  32.8 us
    reduce_scatter x1, waiting for transfers between devices, local(): lax.psum_scatter(partial_value, 'col', scatter_dimension=0, tiled=True)  20.7 us
  transfers between devices with their start and end apart: 2, of which 1 were waited for; matrix products, arithmetic and copies ran while one was open for 0% of the time, Pallas kernels for 0%

profile of v1, /device:TPU:0, one launch (start us, length us, event | category | flops | bytes accessed | tf_op | source)
XLA Modules:
  0.0 115.8 jit_solution(1562504987354502267)
XLA Ops:
  7.2 0.0 copy-start
  7.2 0.0 copy-start.4
  7.2 0.0 reduce-scatter.2.cloned.1.call-start
  7.2 0.8 compare_select_fusion
  8.0 0.0 copy-done.4
  8.0 32.8 %all_gather.9 = f32[16,32,128]{2,1,0:T(8,128)S(1)} all-gather(f32[2,32,128]{2,1,0:T(8,128)} %param.10), channel_id=1, replica_groups=mesh['row'=8,'col'=4] {'row'}, dimensions={0}, use_global_device_ids=true | all-gather | bytes 294912 | tf_op jit(solution)/shard_map/all_gather | solution.py:10
  40.8 0.1 copy.20
  40.9 0.1 reshape.41
  40.9 0.0 copy-start.6
  41.0 0.6 copy-done.6
  41.6 0.1 fusion.7
  41.7 0.1 copy.19
  41.8 0.6 gather_fusion
  42.3 0.0 copy-done
  42.4 0.0 copy-start.3
  42.4 1.9 %convolution_bitcast_fusion = f32[8,32,128]{2,1,0:T(8,128)} fusion(f32[8,2,128,128]{3,2,1,0:T(8,128)S(1)} %copy-done, f32[8,2,32,128]{3,2,1,0:T(8,128)S(1)} %bitcast.11, f32[8,2]{1,0:T(8,128)S(1)} %fusion.7, pred[8,2]{1,0:T(8,128)(4,1)S(1)} %copy.19), kind=kOutput, calls=%fused_computation.1 | convolution fusion | flops 100794368 | bytes 1441872 | tf_op jit(solution)/shard_map/gsab,gsvb->gva/dot_general | solution.py:14
  44.3 0.0 copy-start.1
  44.3 0.0 reduce-scatter.2.cloned.1.call-update
  44.3 0.0 all-reduce.3.cloned.1.call-start
  44.3 20.7 %reduce-scatter.2.cloned.1.call-done = f32[2,32,128]{2,1,0:T(8,128)} async-done(((f32[8,32,128]{2,1,0:T(8,128)}), f32[2,32,128]{2,1,0:T(8,128)}) %reduce-scatter.2.cloned.1.call-update) | async-done | bytes 32784 | tf_op jit(solution)/shard_map/reduce_scatter | solution.py:15
  65.0 0.0 copy-done.3
  65.0 0.9 multiply_reduce_fusion
  65.9 0.0 copy-start.2
  65.9 0.0 copy-done.1
  65.9 0.0 copy-start.5
  65.9 0.2 fusion.13
  66.2 0.4 copy-done.2
  66.5 0.1 copy-done.5
  66.6 1.0 fusion.5
  67.6 0.0 all-reduce.3.cloned.1.call-update
  67.6 0.2 dynamic-update-slice
  67.8 39.3 %all-reduce = f32[1024]{0:T(1024)S(1)} all-reduce(f32[1024]{0:T(1024)S(1)} %dynamic-update-slice), channel_id=2, replica_groups=mesh['row'=8,'col'=4] {'row','col'}, use_global_device_ids=true, to_apply=%add | all-reduce | flops 1024 | bytes 8192
  107.2 0.1 reshape.47
  107.3 0.0 all-reduce.3.cloned.1.call-done
  107.3 1.0 broadcast_divide_fusion
  108.3 0.7 copy.22
  (5 shorter events, 0.1 us)
Async XLA Ops:
  7.2 35.2 %copy-start = (f32[8,2,128,128]{3,2,1,0:T(8,128)S(1)}, f32[8,2,128,128]{3,2,1,0:T(8,128)}, u32[]{:S(2)}) copy-start(f32[8,2,128,128]{3,2,1,0:T(8,128)} %param.7) | copy-start | bytes 3145732
  7.2 0.8 copy-start.4
  7.2 57.8 %reduce-scatter.2.cloned.1.call-start = ((), (), s32[]{:S(2)}) async-start(), calls=%async_computation.1 | async-start | bytes 163840 | tf_op jit(solution)/shard_map/reduce_scatter | solution.py:15
  40.9 0.7 copy-start.6
  42.4 22.7 %copy-start.3 = (f32[2,32,128]{2,1,0:T(8,128)S(1)}, f32[2,32,128]{2,1,0:T(8,128)}, u32[]{:S(2)}) copy-start(f32[2,32,128]{2,1,0:T(8,128)} %param.11) | copy-start | bytes 98308
  44.3 21.7 %copy-start.1 = (f32[2,128,128]{2,1,0:T(8,128)S(1)}, f32[2,128,128]{2,1,0:T(8,128)}, u32[]{:S(2)}) copy-start(f32[2,128,128]{2,1,0:T(8,128)} %param.13) | copy-start | bytes 393220
  44.3 63.0 %all-reduce.3.cloned.1.call-start = ((), (), s32[]{:S(2)}) async-start(), calls=%async_computation.2 | async-start | bytes 262144 | tf_op jit(solution)/shard_map/psum | solution.py:23
  65.9 0.6 copy-start.2
  65.9 0.7 copy-start.5
Sparse Core Ops, SparseCore 0:
  44.4 20.5 reduce-scatter.1
  67.9 31.7 all-reduce.2
